TPU v7x, 32 devices: a whole 2x2x4 slice. The times are simulated.
32 devices in a mesh: gx: 16 (over z, y, x), gy: 1, gz: 2 (over core).
Axes of the slice: x: 2, y: 2, z: 4, core: 2. Of those that a mesh axis runs over, the one named last changes fastest.
Arguments:
- populations: float32 [19, 128, 8, 256], P(None, 'gx', 'gy', 'gz'), may hold values from 0.01 to 0.11
Outputs:
- populations_next: float32 [19, 128, 8, 256], P(None, 'gx', 'gy', 'gz')
- moments_slab: float32 [4, 256, 8, 128], P(None, ('gz', 'gx'), 'gy')
All inputs are finite; a program needn't handle non-finite values.
Results may differ from a plain program's by a relative error of at most 0.0003.
Values sent between devices are 32-bit elements; how exact they have to be, the bound alone decides.
A program may use at most 64 MiB of HBM per device.

v0:
```python
from functools import reduce
import jax
import jax.numpy as jnp
from jax import lax
from jax.sharding import PartitionSpec as P

lattice_moves = [
    (0, 0, 0),
    (1, 0, 0),
    (-1, 0, 0),
    (0, 1, 0),
    (0, -1, 0),
    (0, 0, 1),
    (0, 0, -1),
    (1, 1, 0),
    (-1, -1, 0),
    (1, -1, 0),
    (-1, 1, 0),
    (1, 0, 1),
    (-1, 0, -1),
    (1, 0, -1),
    (-1, 0, 1),
    (0, 1, 1),
    (0, -1, -1),
    (0, 1, -1),
    (0, -1, 1),
]
lattice_weights = [1.0 / 3.0] + [1.0 / 18.0] * 6 + [1.0 / 36.0] * 12
relaxation = 1.6


def with_halo(x, sides, width):
    for axis, dim in sides:
        count, length = (lax.axis_size(axis), x.shape[dim])
        up = [(i, (i + 1) % count) for i in range(count)]
        down = [(j, i) for i, j in up]
        last = lax.slice_in_dim(x, length - width, length, axis=dim)
        leading = lax.slice_in_dim(x, 0, width, axis=dim)
        before = lax.ppermute(last, axis, up)
        after = lax.ppermute(leading, axis, down)
        x = jnp.concatenate([before, x, after], axis=dim)
    return x


def signed_total(pieces, component):
    total = jnp.zeros_like(pieces[0])
    for move, piece in zip(lattice_moves, pieces):
        if move[component] == 1:
            total = total + piece
        elif move[component] == -1:
            total = total - piece
    return total


def lattice_moments(pieces):
    density = reduce(lambda left, right: left + right, pieces)
    velocity_x = signed_total(pieces, 0) / density
    velocity_y = signed_total(pieces, 1) / density
    velocity_z = signed_total(pieces, 2) / density
    return (density, velocity_x, velocity_y, velocity_z)


def collide(pieces):
    density, velocity_x, velocity_y, velocity_z = lattice_moments(pieces)
    speed_sq = velocity_x * velocity_x + velocity_y * velocity_y + velocity_z * velocity_z
    result = []
    for move, weight, piece in zip(lattice_moves, lattice_weights, pieces):
        projected = move[0] * velocity_x + move[1] * velocity_y + move[2] * velocity_z
        balance = (
            weight
            * density
            * (1.0 + 3.0 * projected + 4.5 * projected * projected - 1.5 * speed_sq)
        )
        result.append(piece - relaxation * (piece - balance))
    return result


def stream_axis(pieces, component, padder):
    chosen = [index for index, move in enumerate(lattice_moves) if move[component] != 0]
    padded = padder(jnp.stack([pieces[index] for index in chosen]))
    extent = pieces[0].shape[component]
    result = list(pieces)
    for place, index in enumerate(chosen):
        start = 1 - lattice_moves[index][component]
        result[index] = lax.slice_in_dim(padded[place], start, start + extent, axis=component)
    return result


def on_device(populations):
    pieces = [populations[index] for index in range(19)]
    moments = jnp.stack(lattice_moments(pieces))
    file_order = jnp.transpose(moments, (0, 3, 2, 1))
    moments_slab = lax.all_to_all(file_order, "gx", split_axis=1, concat_axis=3, tiled=True)
    read = stream_axis(pieces, 0, lambda part: with_halo(part, (("gx", 1),), 1))
    read = stream_axis(read, 1, lambda part: with_halo(part, (("gy", 2),), 1))
    read = stream_axis(read, 2, lambda part: with_halo(part, (("gz", 3),), 1))
    populations_next = jnp.stack(collide(read))
    return (populations_next, moments_slab)


def solution(mesh):
    return jax.shard_map(
        on_device,
        mesh=mesh,
        in_specs=(P(None, "gx", "gy", "gz"),),
        out_specs=(P(None, "gx", "gy", "gz"), P(None, ("gz", "gx"), "gy", None)),
        check_vma=False,
    )
```

profile of v0, /device:TPU:0, one launch (start us, length us, event | category | flops | bytes accessed | tf_op | source)
XLA Modules:
  0.0 50.1 jit_solution(12742295588593382738)
XLA Ops:
  0.6 1.0 %slice.286 = f32[8,8,8,128]{3,2,1,0:T(8,128)S(1)} slice(f32[19,8,8,128]{3,2,1,0:T(8,128)} %param.1), slice={[7:15], [0:8], [0:8], [0:128]} | slice | bytes 524288 | tf_op jit(solution)/shard_map/slice | solution.py:90
  1.7 1.5 %constant_dynamic-update-slice_fusion.4 = (f32[10,8,8,128]{3,2,1,0:T(8,128)}, f32[10,8,8,128]{3,2,1,0:T(8,128)S(1)}, f32[2,8,8,128]{3,2,1,0:T(8,128)S(1)}) fusion(f32[19,8,8,128]{3,2,1,0:T(8,128)} %param.1), kind=kLoop, calls=%fused_computation.8 | loop fusion | bytes 393216
  3.2 7.0 %collective-permute-start.1 = (f32[10,1,8,128]{3,2,1,0:T(8,128)S(1)}, f32[10,1,8,128]{3,2,1,0:T(8,128)S(1)}, u32[]{:S(2)}, u32[]{:S(2)}) collective-permute-start(f32[10,1,8,128]{3,2,1,0:T(8,128)S(1)} %get-tuple-element.45), channel_id=1, source_target_pairs={{2,0},{4,2},{6,4},{8,6},{10,8},{12,10},{14,12},{16,14},{18,16},{20... | collective-permute-start | bytes 122888 | tf_op jit(solution)/shard_map/ppermute | solution.py:40
  10.2 1.1 %subtract_divide_fusion.1 = (f32[1,8,8,128]{3,2,1,0:T(8,128)S(1)}, f32[1,8,8,128]{3,2,1,0:T(8,128)S(1)}) fusion(f32[19,8,8,128]{3,2,1,0:T(8,128)} %param.1), kind=kLoop, calls=%fused_computation.241 | loop fusion | flops 229376 | bytes 688128 | tf_op jit(solution)/shard_map/div | solution.py:57
  11.4 0.7 %pad_maximum_fusion.2 = f32[4,8,8,128]{3,2,1,0:T(8,128)} fusion(f32[1,8,8,128]{3,2,1,0:T(8,128)S(1)} %add_divide_fusion, f32[1,8,8,128]{3,2,1,0:T(8,128)S(1)} %subtract_divide_fusion, f32[1,8,8,128]{3,2,1,0:T(8,128)S(1)} %get-tuple-element.4, f32[1,8,8,128]{3,2,1,0:T(8,128)S(1)} %get-tuple-element.5), kind=kLoop, calls=%fused_computation.2 | loop fusion | flops 98304 | bytes 262144 | tf_op jit(solution)/shard_map/stack | solution.py:91
  12.1 2.7 %copy.56 = f32[4,8,8,128]{2,1,0,3:T(8,128)S(1)} copy(f32[4,8,8,128]{3,2,1,0:T(8,128)} %pad_maximum_fusion.2) | data formatting | bytes 262144 | tf_op jit(solution)/shard_map/stack | solution.py:91
  14.8 3.0 %collective-permute-done = f32[10,1,8,128]{3,2,1,0:T(8,128)S(1)} collective-permute-done((f32[10,1,8,128]{3,2,1,0:T(8,128)S(1)}, f32[10,1,8,128]{3,2,1,0:T(8,128)S(1)}, u32[]{:S(2)}, u32[]{:S(2)}) %collective-permute-start) | collective-permute-done | bytes 40992 | tf_op jit(solution)/shard_map/ppermute | solution.py:39
  17.8 0.6 %constant_dynamic-update-slice_fusion.3 = f32[10,8,8,128]{3,2,1,0:T(8,128)} fusion(f32[10,8,8,128]{3,2,1,0:T(8,128)} %get-tuple-element.34, f32[10,1,8,128]{3,2,1,0:T(8,128)S(1)} %collective-permute-done, f32[8,8,8,128]{3,2,1,0:T(8,128)S(1)} %slice.286, f32[2,8,8,128]{3,2,1,0:T(8,128)S(1)} %get-tuple-element.36), kind=kLoop, calls=%fused_computation.7 | loop fusion | flops 16384 | bytes 401408
  19.1 0.6 %constant_dynamic-update-slice_fusion.1 = (f32[10,8,8,128]{3,2,1,0:T(8,128)}, f32[10,8,8,128]{3,2,1,0:T(8,128)S(1)}) fusion(f32[10,8,8,128]{3,2,1,0:T(8,128)} %constant_dynamic-update-slice_fusion.2, f32[10,1,8,128]{3,2,1,0:T(8,128)S(1)} %collective-permute-done, f32[8,8,8,128]{3,2,1,0:T(8,128)S(1)} %slice.286, f32[2,8,8,128]{3,2,1,0:T(8,128)S(1)} %get-tuple-element.36, ...), kind=kLoop, calls=%fused_computation.5 | loop fusion | flops 32768 | bytes 434176
  19.7 0.6 %constant_dynamic-update-slice_fusion = (f32[10,8,8,128]{3,2,1,0:T(8,128)}, f32[10,8,8,128]{3,2,1,0:T(8,128)S(1)}) fusion(f32[10,8,8,128]{3,2,1,0:T(8,128)} %get-tuple-element.39, f32[10,1,8,128]{3,2,1,0:T(8,128)S(1)} %collective-permute-done.1, f32[8,8,8,128]{3,2,1,0:T(8,128)S(1)} %slice.286, f32[2,8,8,128]{3,2,1,0:T(8,128)S(1)} %get-tuple-element.36, ...), kind=kLoop, calls=%fused_computation.4 | loop fusion | flops 32768 | bytes 434176
  20.3 0.7 %slice_dynamic-update-slice_fusion = f32[10,8,8,128]{3,2,1,0:T(8,128)} fusion(f32[10,8,8,128]{3,2,1,0:T(8,128)} %get-tuple-element.37, f32[19,8,8,128]{3,2,1,0:T(8,128)S(1)} %copy-done), kind=kLoop, calls=%fused_computation.3 | loop fusion | bytes 262144 | tf_op jit(solution)/shard_map/stack | solution.py:80
  21.0 1.1 %fusion.152 = (f32[10,8,1,128]{3,2,1,0:T(1,128)S(1)}, f32[10,8,1,128]{3,2,1,0:T(1,128)S(1)}) fusion(f32[10,8,8,128]{3,2,1,0:T(8,128)} %slice_dynamic-update-slice_fusion), kind=kLoop, calls=%fused_computation.254 | loop fusion | bytes 163840 | tf_op jit(solution)/shard_map/slice | solution.py:37
  22.2 1.1 %pad_maximum_fusion = f32[10,8,10,128]{3,2,1,0:T(8,128)S(1)} fusion(f32[10,8,1,128]{3,2,1,0:T(1,128)S(1)} %bitcast.192, f32[10,8,8,128]{3,2,1,0:T(8,128)} %slice_dynamic-update-slice_fusion, f32[10,8,1,128]{3,2,1,0:T(1,128)S(1)} %bitcast.193), kind=kLoop, calls=%fused_computation | loop fusion | flops 204800 | bytes 819200 | tf_op jit(solution)/shard_map/concatenate | solution.py:41
  23.3 0.7 %slice_bitcast_fusion.19 = (f32[8,10,128]{2,1,0:T(8,128)}, f32[8,10,128]{2,1,0:T(8,128)S(1)}, f32[8,10,128]{2,1,0:T(8,128)}, f32[8,10,128]{2,1,0:T(8,128)}, f32[...) fusion(f32[10,8,10,128]{3,2,1,0:T(8,128)S(1)} %pad_maximum_fusion), kind=kLoop, calls=%fused_computation.56 | loop fusion | bytes 819200 | tf_op jit(solution)/shard_map/squeeze | solution.py:85
  24.1 0.9 %fusion.151 = (f32[10,8,8,1]{3,2,1,0:T(8,128)}, f32[10,8,8,1]{3,2,1,0:T(8,128)}) fusion(f32[10,8,8,128]{3,2,1,0:T(8,128)S(1)} %constant_dynamic-update-slice_fusion.5), kind=kLoop, calls=%fused_computation.253 | loop fusion | bytes 10240 | tf_op jit(solution)/shard_map/slice | solution.py:37
  25.5 1.5 %bitcast_bitcast_fusion = f32[128,4,8,8]{3,2,1,0:T(8,128)} fusion(f32[4,8,8,128]{2,1,0,3:T(8,128)S(1)} %copy.56), kind=kLoop, calls=%fused_computation.255 | loop fusion | bytes 262144
  27.0 3.3 %reshape.22 = f32[16,1,2048]{2,1,0:T(1,128)} reshape(f32[128,4,8,8]{3,2,1,0:T(8,128)} %bitcast_bitcast_fusion) | data formatting | bytes 262144
  30.4 4.1 %all-to-all-start = ((f32[16,1,2048]{2,1,0:T(1,128)}), f32[16,1,2048]{2,1,0:T(1,128)S(1)}, u32[]{:S(2)}, u32[]{:S(2)}) async-start(f32[16,1,2048]{2,1,0:T(1,128)} %reshape.22), calls=%async_computation | async-start | bytes 262144 | tf_op jit(solution)/shard_map/all_to_all | solution.py:93
  34.6 1.4 %pad_maximum_fusion.1 = f32[10,8,8,130]{3,2,1,0:T(8,128)S(1)} fusion(f32[10,8,8,1]{3,2,1,0:T(8,128)} %collective-permute-done.5, f32[10,8,8,128]{3,2,1,0:T(8,128)S(1)} %constant_dynamic-update-slice_fusion.5, f32[10,8,8,1]{3,2,1,0:T(8,128)} %collective-permute-done.4), kind=kLoop, calls=%fused_computation.1 | loop fusion | flops 166400 | bytes 665600 | tf_op jit(solution)/shard_map/concatenate | solution.py:41
  37.1 5.3 %all-to-all-done = f32[16,1,2048]{2,1,0:T(1,128)S(1)} async-done(((f32[16,1,2048]{2,1,0:T(1,128)}), f32[16,1,2048]{2,1,0:T(1,128)S(1)}, u32[]{:S(2)}, u32[]{:S(2)}) %all-to-all-start) | async-done | bytes 131104 | tf_op jit(solution)/shard_map/all_to_all | solution.py:93
  42.9 0.9 %reduce = f32[16,2048]{1,0:T(8,128)S(1)} reduce(f32[16,1,2048]{2,1,0:T(1,128)S(1)} %all-to-all-done, f32[]{:T(128)} %broadcast.211), dimensions={1}, to_apply=%all_to_all.13.reduce_sub_computation | reduce | bytes 262148 | tf_op jit(solution)/shard_map/all_to_all | solution.py:93
  43.8 1.1 %reshape.23 = f32[128,4,8,8]{3,2,1,0:T(8,128)S(1)} reshape(f32[16,2048]{1,0:T(8,128)S(1)} %reduce) | data formatting | bytes 262144
  45.0 1.9 %copy.58 = f32[4,8,8,16,8]{4,3,2,1,0:T(8,128)} copy(f32[4,8,8,16,8]{2,4,0,1,3:T(8,128)S(1)} %bitcast.191) | data formatting | bytes 262144 | tf_op jit(solution)/shard_map/all_to_all | solution.py:93
  46.8 3.2 %all_to_all.16 = f32[4,8,8,128]{3,2,1,0:T(8,128)} reshape(f32[4,8,8,16,8]{4,3,2,1,0:T(8,128)} %copy.58) | data formatting | bytes 262144 | tf_op jit(solution)/shard_map/all_to_all | solution.py:93
  (55 shorter events, 2.8 us)
Async XLA Ops:
  0.6 10.7 %copy-start = (f32[19,8,8,128]{3,2,1,0:T(8,128)S(1)}, f32[19,8,8,128]{3,2,1,0:T(8,128)}, u32[]{:S(2)}) copy-start(f32[19,8,8,128]{3,2,1,0:T(8,128)} %param.1) | copy-start | bytes 1867780
  3.2 15.2 %collective-permute-start.1 = (f32[10,1,8,128]{3,2,1,0:T(8,128)S(1)}, f32[10,1,8,128]{3,2,1,0:T(8,128)S(1)}, u32[]{:S(2)}, u32[]{:S(2)}) collective-permute-start(f32[10,1,8,128]{3,2,1,0:T(8,128)S(1)} %get-tuple-element.45), channel_id=1, source_target_pairs={{2,0},{4,2},{6,4},{8,6},{10,8},{12,10},{14,12},{16,14},{18,16},{20... | collective-permute-start | bytes 122888 | tf_op jit(solution)/shard_map/ppermute | solution.py:40
  10.2 7.6 %collective-permute-start = (f32[10,1,8,128]{3,2,1,0:T(8,128)S(1)}, f32[10,1,8,128]{3,2,1,0:T(8,128)S(1)}, u32[]{:S(2)}, u32[]{:S(2)}) collective-permute-start(f32[10,1,8,128]{3,2,1,0:T(8,128)S(1)} %get-tuple-element.46), channel_id=1, source_target_pairs={{0,2},{2,4},{4,6},{6,8},{8,10},{10,12},{12,14},{14,16},{16,18},{18... | collective-permute-start | bytes 122888 | tf_op jit(solution)/shard_map/ppermute | solution.py:39
  22.1 0.1 collective-permute-start.3
  22.1 0.1 collective-permute-start.2
  25.0 9.5 %collective-permute-start.4 = (f32[10,8,8,1]{3,2,1,0:T(8,128)}, f32[10,8,8,1]{3,2,1,0:T(8,128)}, u32[]{:S(2)}, u32[]{:S(2)}) collective-permute-start(f32[10,8,8,1]{3,2,1,0:T(8,128)} %get-tuple-element.41), channel_id=1, source_target_pairs={{0,1},{1,0},{2,3},{3,2},{4,5},{5,4},{6,7},{7,6},{8,9},{9,8},{10,11... | collective-permute-start | bytes 7688 | tf_op jit(solution)/shard_map/ppermute | solution.py:39
  25.0 9.5 %collective-permute-start.5 = (f32[10,8,8,1]{3,2,1,0:T(8,128)}, f32[10,8,8,1]{3,2,1,0:T(8,128)}, u32[]{:S(2)}, u32[]{:S(2)}) collective-permute-start(f32[10,8,8,1]{3,2,1,0:T(8,128)} %get-tuple-element.42), channel_id=1, source_target_pairs={{1,0},{0,1},{3,2},{2,3},{5,4},{4,5},{7,6},{6,7},{9,8},{8,9},{11,10... | collective-permute-start | bytes 7688 | tf_op jit(solution)/shard_map/ppermute | solution.py:40
  30.4 5.6 %copy-start.1 = (f32[8,10,128]{2,1,0:T(8,128)S(1)}, f32[8,10,128]{2,1,0:T(8,128)}, u32[]{:S(2)}) copy-start(f32[8,10,128]{2,1,0:T(8,128)} %get-tuple-element.26) | copy-start | bytes 122884
  30.4 5.6 %copy-start.2 = (f32[8,10,128]{2,1,0:T(8,128)S(1)}, f32[8,10,128]{2,1,0:T(8,128)}, u32[]{:S(2)}) copy-start(f32[8,10,128]{2,1,0:T(8,128)} %get-tuple-element.27) | copy-start | bytes 122884
  30.4 5.6 %copy-start.3 = (f32[8,10,128]{2,1,0:T(8,128)S(1)}, f32[8,10,128]{2,1,0:T(8,128)}, u32[]{:S(2)}) copy-start(f32[8,10,128]{2,1,0:T(8,128)} %get-tuple-element.28) | copy-start | bytes 122884
  30.4 5.7 %copy-start.4 = (f32[8,10,128]{2,1,0:T(8,128)S(1)}, f32[8,10,128]{2,1,0:T(8,128)}, u32[]{:S(2)}) copy-start(f32[8,10,128]{2,1,0:T(8,128)} %get-tuple-element.33) | copy-start | bytes 122884
  30.4 5.7 %copy-start.5 = (f32[8,10,128]{2,1,0:T(8,128)S(1)}, f32[8,10,128]{2,1,0:T(8,128)}, u32[]{:S(2)}) copy-start(f32[8,10,128]{2,1,0:T(8,128)} %get-tuple-element.24) | copy-start | bytes 122884
  30.4 11.9 %all-to-all-start = ((f32[16,1,2048]{2,1,0:T(1,128)}), f32[16,1,2048]{2,1,0:T(1,128)S(1)}, u32[]{:S(2)}, u32[]{:S(2)}) async-start(f32[16,1,2048]{2,1,0:T(1,128)} %reshape.22), calls=%async_computation | async-start | bytes 262144 | tf_op jit(solution)/shard_map/all_to_all | solution.py:93
  37.1 5.8 %copy-start.6 = (f32[19,8,8,128]{3,2,1,0:T(8,128)}, f32[19,8,8,128]{3,2,1,0:T(8,128)S(1)}, u32[]{:S(2)}) copy-start(f32[19,8,8,128]{3,2,1,0:T(8,128)S(1)} %constant_dynamic-update-slice_fusion.14) | copy-start | bytes 1867780
where the time goes:
time: 50.6 us; the launch traced here: 50.1 us
  local copies, waits for them, and re-layouts  20.5 us (41%)
  starting transfers between devices  11.7 us (23%)
  other arithmetic  8.69 us (17%)
  waiting for transfers between devices  8.31 us (16%)
  between operations  0.93 us (2%)
    unnamed x21, local copies, waits for them, and re-layouts  7.58 us
    ppermute x3, starting transfers between devices, with_halo(): after = lax.ppermute(leading, axis, down)  7.52 us
    all_to_all x3, local copies, waits for them, and re-layouts, on_device(): lax.all_to_all(file_order, 'gx', split_axis=1, concat_axis=3, tiled=True)  5.64 us
    all_to_all x1, waiting for transfers between devices, on_device(): lax.all_to_all(file_order, 'gx', split_axis=1, concat_axis=3, tiled=True)  5.26 us
    all_to_all x1, starting transfers between devices, on_device(): lax.all_to_all(file_order, 'gx', split_axis=1, concat_axis=3, tiled=True)  4.12 us
    unnamed x24, other arithmetic  3.4 us
    ppermute x3, waiting for transfers between devices, with_halo(): before = lax.ppermute(last, axis, up)  3.04 us
    another operation x1, local copies, waits for them, and re-layouts, on_device(): moments = jnp.stack(lattice_moments(pieces))  2.72 us
  transfers between devices with their start and end apart: 7, of which 2 were waited for; matrix products, arithmetic and copies ran while one was open for 25% of the time, Pallas kernels for 0%

commit v1 on v0

--- a/solution.py
+++ b/solution.py
@@ -90,7 +90,10 @@
     pieces = [populations[index] for index in range(19)]
     moments = jnp.stack(lattice_moments(pieces))
     file_order = jnp.transpose(moments, (0, 3, 2, 1))
-    moments_slab = lax.all_to_all(file_order, "gx", split_axis=1, concat_axis=3, tiled=True)
+    moments_slab = jnp.concatenate(
+        lax.all_to_all(jnp.stack(jnp.split(file_order, lax.axis_size("gx"), axis=1)), "gx", 0, 0),
+        axis=3,
+    )
     read = stream_axis(pieces, 0, lambda part: with_halo(part, (("gx", 1),), 1))
     read = stream_axis(read, 1, lambda part: with_halo(part, (("gy", 2),), 1))
     read = stream_axis(read, 2, lambda part: with_halo(part, (("gz", 3),), 1))

time: 50.6 us -> 40.1 us (0.79)
  local copies, waits for them, and re-layouts: 20.5 us -> 14.6 us
  other arithmetic: 8.69 us -> 4.61 us
  waiting for transfers between devices: 8.31 us -> 5.28 us
  starting transfers between devices: 11.7 us -> 14 us
    reshape x0 -> x3, local copies, waits for them, and re-layouts: none -> 6.01 us  [on_device(): jnp.concatenate(lax.all_to_all(jnp.stack(jnp.split(file_order, lax.axis_s...]
    all_to_all x3 -> x1, local copies, waits for them, and re-layouts: 5.64 us -> 0.51 us  [on_device(): lax.all_to_all(jnp.stack(jnp.split(file_order, lax.axis_size('gx'), axis=...]
    ppermute x3, waiting for transfers between devices: 3.04 us -> 0.01 us  [with_halo(): before = lax.ppermute(last, axis, up)]
    ppermute x3, starting transfers between devices: 0.01 us -> 3.03 us  [with_halo(): before = lax.ppermute(last, axis, up)]
    ppermute x3, starting transfers between devices: 7.52 us -> 4.57 us  [with_halo(): after = lax.ppermute(leading, axis, down)]
    another operation x1, local copies, waits for them, and re-layouts: 2.72 us -> 0.09 us  [on_device(): jnp.stack(jnp.split(file_order, lax.axis_size('gx'), axis=1))]
    unnamed x24, other arithmetic: 3.4 us -> 0.96 us
    unnamed x21 -> x35, local copies, waits for them, and re-layouts: 7.58 us -> 5.24 us
  transfers between devices with their start and end apart: 7 -> 7, of which waited for: 2 -> 1; matrix products, arithmetic and copies ran while one was open for 25% -> 17% of each run, Pallas kernels for 0% -> 0%
where the time goes in v1:
time: 40.1 us; the launch traced here: 39.6 us
  local copies, waits for them, and re-layouts  14.6 us (36%)
  starting transfers between devices  14 us (35%)
  waiting for transfers between devices  5.28 us (13%)
  other arithmetic  4.61 us (11%)
  between operations  1.12 us (3%)
    all_to_all x1, starting transfers between devices, on_device(): lax.all_to_all(jnp.stack(jnp.split(file_order, lax.axis_size('gx'), axis=...  6.42 us
    reshape x3, local copies, waits for them, and re-layouts, on_device(): jnp.concatenate(lax.all_to_all(jnp.stack(jnp.split(file_order, lax.axis_s...  6.01 us
    all_to_all x1, waiting for transfers between devices, on_device(): lax.all_to_all(jnp.stack(jnp.split(file_order, lax.axis_size('gx'), axis=...  5.27 us
    unnamed x35, local copies, waits for them, and re-layouts  5.24 us
    ppermute x3, starting transfers between devices, with_halo(): after = lax.ppermute(leading, axis, down)  4.57 us
    ppermute x3, starting transfers between devices, with_halo(): before = lax.ppermute(last, axis, up)  3.03 us
    concatenate x2, other arithmetic, with_halo(): x = jnp.concatenate([before, x, after], axis=dim)  1.52 us
    div x1, other arithmetic, lattice_moments(): velocity_x = signed_total(pieces, 0) / density  1.09 us
  transfers between devices with their start and end apart: 7, of which 1 were waited for; matrix products, arithmetic and copies ran while one was open for 17% of the time, Pallas kernels for 0%

profile of v1, /device:TPU:0, one launch (start us, length us, event | category | flops | bytes accessed | tf_op | source)
XLA Modules:
  0.0 39.6 jit_solution(14383960465926394549)
XLA Ops:
  0.6 1.0 %constant_dynamic-update-slice_fusion.4 = (f32[10,8,8,128]{3,2,1,0:T(8,128)S(1)}, f32[10,8,8,128]{3,2,1,0:T(8,128)S(1)}, f32[2,8,8,128]{3,2,1,0:T(8,128)S(1)}) fusion(f32[19,8,8,128]{3,2,1,0:T(8,128)} %param.1), kind=kLoop, calls=%fused_computation.40 | loop fusion | bytes 393216
  1.6 1.0 %slice.286 = f32[8,8,8,128]{3,2,1,0:T(8,128)S(1)} slice(f32[19,8,8,128]{3,2,1,0:T(8,128)} %param.1), slice={[7:15], [0:8], [0:8], [0:128]} | slice | bytes 524288 | tf_op jit(solution)/shard_map/slice | solution.py:90
  2.6 3.0 %collective-permute-start = (f32[10,1,8,128]{3,2,1,0:T(8,128)S(1)}, f32[10,1,8,128]{3,2,1,0:T(8,128)S(1)}, u32[]{:S(2)}, u32[]{:S(2)}) collective-permute-start(f32[10,1,8,128]{3,2,1,0:T(8,128)S(1)} %get-tuple-element.44), channel_id=1, source_target_pairs={{0,2},{2,4},{4,6},{6,8},{8,10},{10,12},{12,14},{14,16},{16,18},{18... | collective-permute-start | bytes 122888 | tf_op jit(solution)/shard_map/ppermute | solution.py:39
  5.6 4.1 %collective-permute-start.1 = (f32[10,1,8,128]{3,2,1,0:T(8,128)S(1)}, f32[10,1,8,128]{3,2,1,0:T(8,128)S(1)}, u32[]{:S(2)}, u32[]{:S(2)}) collective-permute-start(f32[10,1,8,128]{3,2,1,0:T(8,128)S(1)} %get-tuple-element.43), channel_id=1, source_target_pairs={{2,0},{4,2},{6,4},{8,6},{10,8},{12,10},{14,12},{16,14},{18,16},{20... | collective-permute-start | bytes 122888 | tf_op jit(solution)/shard_map/ppermute | solution.py:40
  9.7 1.1 %subtract_divide_fusion.1 = (f32[1,8,8,128]{3,2,1,0:T(8,128)S(1)}, f32[1,8,8,128]{3,2,1,0:T(8,128)S(1)}) fusion(f32[19,8,8,128]{3,2,1,0:T(8,128)} %param.1), kind=kLoop, calls=%fused_computation.273 | loop fusion | flops 229376 | bytes 688128 | tf_op jit(solution)/shard_map/div | solution.py:57
  11.0 0.1 fusion.13
  11.4 0.1 fusion.9
  11.5 0.1 fusion.8
  11.8 0.1 fusion.5
  12.6 0.1 pad_maximum_fusion
  12.7 0.7 %slice_bitcast_fusion.35 = (f32[8,10,128]{2,1,0:T(8,128)}, f32[8,10,128]{2,1,0:T(8,128)S(1)}, f32[8,10,128]{2,1,0:T(8,128)}, f32[8,10,128]{2,1,0:T(8,128)}, f32[...) fusion(f32[10,8,10,128]{3,2,1,0:T(8,128)S(1)} %pad_maximum_fusion), kind=kLoop, calls=%fused_computation.88 | loop fusion | bytes 819200 | tf_op jit(solution)/shard_map/squeeze | solution.py:85
  13.5 0.9 %fusion.167 = (f32[10,8,8,1]{3,2,1,0:T(8,128)}, f32[10,8,8,1]{3,2,1,0:T(8,128)}) fusion(f32[10,8,8,128]{3,2,1,0:T(8,128)S(1)} %constant_dynamic-update-slice_fusion.5), kind=kLoop, calls=%fused_computation.285 | loop fusion | bytes 10240 | tf_op jit(solution)/shard_map/slice | solution.py:37
  14.4 0.5 %collective-permute-start.5 = (f32[10,8,8,1]{3,2,1,0:T(8,128)}, f32[10,8,8,1]{3,2,1,0:T(8,128)}, u32[]{:S(2)}, u32[]{:S(2)}) collective-permute-start(f32[10,8,8,1]{3,2,1,0:T(8,128)} %get-tuple-element.40), channel_id=1, source_target_pairs={{1,0},{0,1},{3,2},{2,3},{5,4},{4,5},{7,6},{6,7},{9,8},{8,9},{11,10... | collective-permute-start | bytes 7688 | tf_op jit(solution)/shard_map/ppermute | solution.py:40
  15.0 1.7 %reshape.30 = f32[16,1,2048]{2,1,0:T(1,128)} reshape(f32[16,4,8,8,8]{4,3,2,1,0:T(8,128)S(1)} %bitcast.249) | data formatting | bytes 262144
  16.8 6.4 %all-to-all-start = ((f32[16,1,2048]{2,1,0:T(1,128)}), f32[16,1,2048]{2,1,0:T(1,128)S(1)}, u32[]{:S(2)}, u32[]{:S(2)}) async-start(f32[16,1,2048]{2,1,0:T(1,128)} %reshape.30), calls=%async_computation | async-start | bytes 262144 | tf_op jit(solution)/shard_map/all_to_all | solution.py:94
  23.2 1.4 %pad_maximum_fusion.1 = f32[10,8,8,130]{3,2,1,0:T(8,128)S(1)} fusion(f32[10,8,8,1]{3,2,1,0:T(8,128)} %collective-permute-done.5, f32[10,8,8,128]{3,2,1,0:T(8,128)S(1)} %constant_dynamic-update-slice_fusion.5, f32[10,8,8,1]{3,2,1,0:T(8,128)} %collective-permute-done.4), kind=kLoop, calls=%fused_computation.1 | loop fusion | flops 166400 | bytes 665600 | tf_op jit(solution)/shard_map/concatenate | solution.py:41
  24.7 0.2 constant_dynamic-update-slice_fusion.32
  25.7 5.3 %all-to-all-done = f32[16,1,2048]{2,1,0:T(1,128)S(1)} async-done(((f32[16,1,2048]{2,1,0:T(1,128)}), f32[16,1,2048]{2,1,0:T(1,128)S(1)}, u32[]{:S(2)}, u32[]{:S(2)}) %all-to-all-start) | async-done | bytes 131104 | tf_op jit(solution)/shard_map/all_to_all | solution.py:94
  31.0 0.5 %broadcast.211 = f32[]{:T(128)} broadcast(f32[]{:T(128)} %constant.379), dimensions={} | broadcast | bytes 8 | tf_op jit(solution)/shard_map/all_to_all | solution.py:94
  31.5 0.9 %reduce = f32[16,2048]{1,0:T(8,128)S(1)} reduce(f32[16,1,2048]{2,1,0:T(1,128)S(1)} %all-to-all-done, f32[]{:T(128)} %broadcast.211), dimensions={1}, to_apply=%all_to_all.3.reduce_sub_computation | reduce | bytes 262148 | tf_op jit(solution)/shard_map/all_to_all | solution.py:94
  32.5 1.1 %reshape.31 = f32[16,4,8,8,8]{4,3,2,1,0:T(8,128)S(1)} reshape(f32[16,2048]{1,0:T(8,128)S(1)} %reduce) | data formatting | bytes 262144
  33.6 1.5 %bitcast_bitcast_fusion = f32[4,8,8,16,8]{1,2,4,0,3:T(8,128)} fusion(f32[16,4,8,8,8]{4,3,2,1,0:T(8,128)S(1)} %reshape.31), kind=kLoop, calls=%fused_computation.287 | loop fusion | bytes 262144 | tf_op jit(solution)/shard_map/reshape | solution.py:93
  35.1 2.9 %copy.4 = f32[4,8,8,16,8]{4,3,2,1,0:T(8,128)S(1)} copy(f32[4,8,8,16,8]{1,2,4,0,3:T(8,128)} %bitcast_bitcast_fusion) | data formatting | bytes 262144 | tf_op jit(solution)/shard_map/reshape | solution.py:93
  38.0 1.6 %reshape.29 = f32[4,8,8,128]{3,2,1,0:T(8,128)} reshape(f32[4,8,8,16,8]{4,3,2,1,0:T(8,128)S(1)} %copy.4) | data formatting | bytes 262144 | tf_op jit(solution)/shard_map/reshape | solution.py:93
  (70 shorter events, 2.1 us)
Async XLA Ops:
  0.6 10.2 %copy-start = (f32[19,8,8,128]{3,2,1,0:T(8,128)S(1)}, f32[19,8,8,128]{3,2,1,0:T(8,128)}, u32[]{:S(2)}) copy-start(f32[19,8,8,128]{3,2,1,0:T(8,128)} %param.1) | copy-start | bytes 1867780
  2.6 9.7 %collective-permute-start = (f32[10,1,8,128]{3,2,1,0:T(8,128)S(1)}, f32[10,1,8,128]{3,2,1,0:T(8,128)S(1)}, u32[]{:S(2)}, u32[]{:S(2)}) collective-permute-start(f32[10,1,8,128]{3,2,1,0:T(8,128)S(1)} %get-tuple-element.44), channel_id=1, source_target_pairs={{0,2},{2,4},{4,6},{6,8},{8,10},{10,12},{12,14},{14,16},{16,18},{18... | collective-permute-start | bytes 122888 | tf_op jit(solution)/shard_map/ppermute | solution.py:39
  5.6 6.7 %collective-permute-start.1 = (f32[10,1,8,128]{3,2,1,0:T(8,128)S(1)}, f32[10,1,8,128]{3,2,1,0:T(8,128)S(1)}, u32[]{:S(2)}, u32[]{:S(2)}) collective-permute-start(f32[10,1,8,128]{3,2,1,0:T(8,128)S(1)} %get-tuple-element.43), channel_id=1, source_target_pairs={{2,0},{4,2},{6,4},{8,6},{10,8},{12,10},{14,12},{16,14},{18,16},{20... | collective-permute-start | bytes 122888 | tf_op jit(solution)/shard_map/ppermute | solution.py:40
  12.5 0.1 collective-permute-start.2
  12.5 0.1 collective-permute-start.3
  14.4 8.8 %collective-permute-start.4 = (f32[10,8,8,1]{3,2,1,0:T(8,128)}, f32[10,8,8,1]{3,2,1,0:T(8,128)}, u32[]{:S(2)}, u32[]{:S(2)}) collective-permute-start(f32[10,8,8,1]{3,2,1,0:T(8,128)} %get-tuple-element.39), channel_id=1, source_target_pairs={{0,1},{1,0},{2,3},{3,2},{4,5},{5,4},{6,7},{7,6},{8,9},{9,8},{10,11... | collective-permute-start | bytes 7688 | tf_op jit(solution)/shard_map/ppermute | solution.py:39
  14.4 8.8 %collective-permute-start.5 = (f32[10,8,8,1]{3,2,1,0:T(8,128)}, f32[10,8,8,1]{3,2,1,0:T(8,128)}, u32[]{:S(2)}, u32[]{:S(2)}) collective-permute-start(f32[10,8,8,1]{3,2,1,0:T(8,128)} %get-tuple-element.40), channel_id=1, source_target_pairs={{1,0},{0,1},{3,2},{2,3},{5,4},{4,5},{7,6},{6,7},{9,8},{8,9},{11,10... | collective-permute-start | bytes 7688 | tf_op jit(solution)/shard_map/ppermute | solution.py:40
  16.8 7.9 %copy-start.1 = (f32[8,10,128]{2,1,0:T(8,128)S(1)}, f32[8,10,128]{2,1,0:T(8,128)}, u32[]{:S(2)}) copy-start(f32[8,10,128]{2,1,0:T(8,128)} %get-tuple-element.24) | copy-start | bytes 122884
  16.8 7.9 %copy-start.2 = (f32[8,10,128]{2,1,0:T(8,128)S(1)}, f32[8,10,128]{2,1,0:T(8,128)}, u32[]{:S(2)}) copy-start(f32[8,10,128]{2,1,0:T(8,128)} %get-tuple-element.25) | copy-start | bytes 122884
  16.8 7.9 %copy-start.3 = (f32[8,10,128]{2,1,0:T(8,128)S(1)}, f32[8,10,128]{2,1,0:T(8,128)}, u32[]{:S(2)}) copy-start(f32[8,10,128]{2,1,0:T(8,128)} %get-tuple-element.26) | copy-start | bytes 122884
  16.8 8.0 %copy-start.4 = (f32[8,10,128]{2,1,0:T(8,128)S(1)}, f32[8,10,128]{2,1,0:T(8,128)}, u32[]{:S(2)}) copy-start(f32[8,10,128]{2,1,0:T(8,128)} %get-tuple-element.31) | copy-start | bytes 122884
  16.8 8.0 %copy-start.5 = (f32[8,10,128]{2,1,0:T(8,128)S(1)}, f32[8,10,128]{2,1,0:T(8,128)}, u32[]{:S(2)}) copy-start(f32[8,10,128]{2,1,0:T(8,128)} %get-tuple-element.22) | copy-start | bytes 122884
  16.8 14.2 %all-to-all-start = ((f32[16,1,2048]{2,1,0:T(1,128)}), f32[16,1,2048]{2,1,0:T(1,128)S(1)}, u32[]{:S(2)}, u32[]{:S(2)}) async-start(f32[16,1,2048]{2,1,0:T(1,128)} %reshape.30), calls=%async_computation | async-start | bytes 262144 | tf_op jit(solution)/shard_map/all_to_all | solution.py:94
  25.7 9.4 %copy-start.6 = (f32[19,8,8,128]{3,2,1,0:T(8,128)}, f32[19,8,8,128]{3,2,1,0:T(8,128)S(1)}, u32[]{:S(2)}) copy-start(f32[19,8,8,128]{3,2,1,0:T(8,128)S(1)} %constant_dynamic-update-slice_fusion.14) | copy-start | bytes 1867780
